TPU v7x, 32 devices: a whole 2x2x4 slice. The times are simulated.
32 devices in a mesh: dp: 2 (over x), cols: 4 (over z), rows: 4 (over y, core).
Axes of the slice: x: 2, y: 2, z: 4, core: 2. Of those that a mesh axis runs over, the one named last changes fastest.
Arguments:
- h_init: bfloat16 [2, 96, 96, 256], P('dp', 'rows', 'cols'), parts along dimension 0
- c_init: float32 [2, 96, 96, 256], P('dp', 'rows', 'cols'), parts along dimension 0
- w_rec: bfloat16 [3, 3, 256, 1024], replicated
- gate_bias: float32 [24, 1024], replicated
Outputs:
- output 1: bfloat16 [24, 2, 96, 96, 256], P(None, 'dp', 'rows', 'cols'), parts along dimension 1
- output 2: float32 [2, 96, 96, 256], P('dp', 'rows', 'cols'), parts along dimension 0
There are 2 independent parts. A program takes and returns all parts, laid end to end along the dimension named above; an argument that names none is the same for every part.
All inputs are finite; a program needn't handle non-finite values.
Results may differ from a plain program's by a relative error of at most 0.00408108.
Values are sent between devices in bfloat16 or wider.
A program may use at most 1 GiB of HBM per device.

v0:
```python
import jax
import jax.numpy as jnp
from jax import lax
from jax.sharding import PartitionSpec as P


def lstm_update(gate_pre, c_prev):
    in_gate, forget_gate, out_gate, cand_gate = jnp.split(gate_pre, 4, axis=-1)
    c_next = jax.nn.sigmoid(forget_gate) * c_prev + jax.nn.sigmoid(in_gate) * jnp.tanh(cand_gate)
    h_next = (jax.nn.sigmoid(out_gate) * jnp.tanh(c_next)).astype(jnp.bfloat16)
    return h_next, c_next


def solution(mesh):
    row_count = mesh.shape["rows"]
    col_count = mesh.shape["cols"]
    rows_down = [(src_pos, src_pos + 1) for src_pos in range(row_count - 1)]
    rows_up = [(src_pos + 1, src_pos) for src_pos in range(row_count - 1)]
    cols_right = [(src_pos, src_pos + 1) for src_pos in range(col_count - 1)]
    cols_left = [(src_pos + 1, src_pos) for src_pos in range(col_count - 1)]

    def with_halo(tile):
        from_above = lax.ppermute(tile[:, -1:], "rows", rows_down)
        from_below = lax.ppermute(tile[:, :1], "rows", rows_up)
        tall_tile = jnp.concatenate([from_above, tile, from_below], axis=1)
        from_left = lax.ppermute(tall_tile[:, :, -1:], "cols", cols_right)
        from_right = lax.ppermute(tall_tile[:, :, :1], "cols", cols_left)
        return jnp.concatenate([from_left, tall_tile, from_right], axis=2)

    def device_fn(h_init, c_init, w_rec, gate_bias):
        def one_step(carry_in, bias_row):
            h_prev, c_prev = carry_in
            padded = with_halo(h_prev)
            gate_pre = lax.conv_general_dilated(padded, w_rec, (1, 1), "VALID", dimension_numbers=("NHWC", "HWIO", "NHWC"), preferred_element_type=jnp.float32) + bias_row
            h_next, c_next = lstm_update(gate_pre, c_prev)
            return (h_next, c_next), h_next

        final_state, h_seq = lax.scan(one_step, (h_init, c_init), gate_bias)
        return h_seq, final_state[1]

    state_spec = P("dp", "rows", "cols", None)
    return jax.shard_map(device_fn, mesh=mesh, in_specs=(state_spec, state_spec, P(), P()), out_specs=(P(None, "dp", "rows", "cols", None), state_spec), check_vma=False)
```

profile of v0, /device:TPU:0, one launch (start us, length us, event | category | flops | bytes accessed | tf_op | source)
XLA Modules:
  0.0 583.2 jit_solution(10845919159838904843)
XLA Ops:
  2.9 579.3 %while.14 = (s32[]{:T(128)}, bf16[1,24,24,256]{3,1,2,0:T(8,128)(2,1)S(1)}, f32[1,24,24,256]{3,1,2,0:T(8,128)S(1)}, bf16[24,1,24,24,256]{4,3,2,1,0:T(8,128)(2,1)}...) while((s32[]{:T(128)}, ...), condition=%wide.region_1.2_spmd, body=%wide.region_0.1_spmd.sunk | while | flops 3631734784 | bytes 25835980 | solution.py:38
  9.5 5.6 collective-permute-start.3
  17.2 5.7 select_add_fusion.2
  32.7 4.8 collective-permute-start.3
  39.5 5.7 select_add_fusion.2
  49.8 5.2 collective-permute-start.1
  63.8 5.7 select_add_fusion.2
  74.1 5.2 collective-permute-start.1
  81.5 4.6 collective-permute-start.3
  88.1 5.7 select_add_fusion.2
  98.4 5.2 collective-permute-start.1
  105.7 4.5 collective-permute-start.3
  112.3 5.7 select_add_fusion.2
  122.6 5.2 collective-permute-start.1
  130.0 4.5 collective-permute-start.3
  136.6 5.7 select_add_fusion.2
  146.9 5.2 collective-permute-start.1
  154.3 4.5 collective-permute-start.3
  160.9 5.7 select_add_fusion.2
  171.1 5.2 collective-permute-start.1
  178.5 4.5 collective-permute-start.3
  185.1 5.7 select_add_fusion.2
  195.4 5.2 collective-permute-start.1
  202.8 4.5 collective-permute-start.3
  209.4 5.7 select_add_fusion.2
  219.7 5.2 collective-permute-start.1
  227.0 4.5 collective-permute-start.3
  233.7 5.7 select_add_fusion.2
  243.9 5.2 collective-permute-start.1
  251.3 4.5 collective-permute-start.3
  257.9 5.7 select_add_fusion.2
  268.2 5.2 collective-permute-start.1
  275.6 4.5 collective-permute-start.3
  282.2 5.7 select_add_fusion.2
  292.4 5.2 collective-permute-start.1
  299.8 4.5 collective-permute-start.3
  306.4 5.7 select_add_fusion.2
  316.7 5.2 collective-permute-start.1
  324.1 4.5 collective-permute-start.3
  330.7 5.7 select_add_fusion.2
  341.0 5.2 collective-permute-start.1
  348.3 4.5 collective-permute-start.3
  355.0 5.7 select_add_fusion.2
  365.2 5.2 collective-permute-start.1
  372.6 4.5 collective-permute-start.3
  379.2 5.7 select_add_fusion.2
  389.5 5.2 collective-permute-start.1
  396.9 4.5 collective-permute-start.3
  403.5 5.7 select_add_fusion.2
  413.8 5.2 collective-permute-start.1
  421.1 4.5 collective-permute-start.3
  427.7 5.7 select_add_fusion.2
  438.0 5.2 collective-permute-start.1
  452.0 5.7 select_add_fusion.2
  462.3 5.2 collective-permute-start.1
  476.3 5.7 select_add_fusion.2
  486.5 5.2 collective-permute-start.1
  500.5 5.7 select_add_fusion.2
  510.8 5.2 collective-permute-start.1
  524.8 5.7 select_add_fusion.2
  535.1 5.2 collective-permute-start.1
  549.0 5.7 select_add_fusion.2
  559.3 5.2 collective-permute-start.1
  573.3 5.7 select_add_fusion.2
  (517 shorter events, 249.9 us)
Async XLA Ops:
  8.2 7.7 %collective-permute-start.2 = (bf16[1,26,1,256]{3,1,2,0:T(8,128)(2,1)S(1)}, bf16[1,26,1,256]{3,1,2,0:T(8,128)(2,1)S(1)}, u32[]{:S(2)}, u32[]{:S(2)}) collective-permute-start(bf16[1,26,1,256]{3,1,2,0:T(8,128)(2,1)S(1)} %get-tuple-element.114), channel_id=1, source_target_pairs={{4,0},{8,4},{12,8},{5,1},{9,5},{13,9},{6,2},{10,6},{14,10},{7,3},{... | collective-permute-start | bytes 39944 | tf_op jit(solution)/shard_map/while/body/eval_jaxpr/ppermute | solution.py:27
  9.5 7.0 %collective-permute-start.3 = (bf16[1,26,1,256]{3,1,2,0:T(8,128)(2,1)S(1)}, bf16[1,26,1,256]{3,1,2,0:T(8,128)(2,1)S(1)}, u32[]{:S(2)}, u32[]{:S(2)}) collective-permute-start(bf16[1,26,1,256]{3,1,2,0:T(8,128)(2,1)S(1)} %get-tuple-element.115), channel_id=1, source_target_pairs={{0,4},{4,8},{8,12},{1,5},{5,9},{9,13},{2,6},{6,10},{10,14},{3,7},{... | collective-permute-start | bytes 39944 | tf_op jit(solution)/shard_map/while/body/eval_jaxpr/ppermute | solution.py:26
  31.4 6.9 %collective-permute-start.2 = (bf16[1,26,1,256]{3,1,2,0:T(8,128)(2,1)S(1)}, bf16[1,26,1,256]{3,1,2,0:T(8,128)(2,1)S(1)}, u32[]{:S(2)}, u32[]{:S(2)}) collective-permute-start(bf16[1,26,1,256]{3,1,2,0:T(8,128)(2,1)S(1)} %get-tuple-element.114), channel_id=1, source_target_pairs={{4,0},{8,4},{12,8},{5,1},{9,5},{13,9},{6,2},{10,6},{14,10},{7,3},{... | collective-permute-start | bytes 39944 | tf_op jit(solution)/shard_map/while/body/eval_jaxpr/ppermute | solution.py:27
  32.7 6.2 %collective-permute-start.3 = (bf16[1,26,1,256]{3,1,2,0:T(8,128)(2,1)S(1)}, bf16[1,26,1,256]{3,1,2,0:T(8,128)(2,1)S(1)}, u32[]{:S(2)}, u32[]{:S(2)}) collective-permute-start(bf16[1,26,1,256]{3,1,2,0:T(8,128)(2,1)S(1)} %get-tuple-element.115), channel_id=1, source_target_pairs={{0,4},{4,8},{8,12},{1,5},{5,9},{9,13},{2,6},{6,10},{10,14},{3,7},{... | collective-permute-start | bytes 39944 | tf_op jit(solution)/shard_map/while/body/eval_jaxpr/ppermute | solution.py:26
  48.5 6.6 %collective-permute-start = (bf16[1,1,24,256]{3,1,2,0:T(2,128)(2,1)S(1)}, bf16[1,1,24,256]{3,1,2,0:T(2,128)(2,1)S(1)}, u32[]{:S(2)}, u32[]{:S(2)}) collective-permute-start(bf16[1,1,24,256]{3,1,2,0:T(2,128)(2,1)S(1)} %get-tuple-element.112), channel_id=1, source_target_pairs={{1,0},{2,1},{3,2},{5,4},{6,5},{7,6},{9,8},{10,9},{11,10},{13,12},{... | collective-permute-start | bytes 36872 | tf_op jit(solution)/shard_map/while/body/eval_jaxpr/ppermute | solution.py:24
  49.8 6.1 %collective-permute-start.1 = (bf16[1,1,24,256]{3,1,2,0:T(2,128)(2,1)S(1)}, bf16[1,1,24,256]{3,1,2,0:T(2,128)(2,1)S(1)}, u32[]{:S(2)}, u32[]{:S(2)}) collective-permute-start(bf16[1,1,24,256]{3,1,2,0:T(2,128)(2,1)S(1)} %get-tuple-element.113), channel_id=1, source_target_pairs={{0,1},{1,2},{2,3},{4,5},{5,6},{6,7},{8,9},{9,10},{10,11},{12,13},{... | collective-permute-start | bytes 36872 | tf_op jit(solution)/shard_map/while/body/eval_jaxpr/ppermute | solution.py:23
  55.9 6.6 %collective-permute-start.2 = (bf16[1,26,1,256]{3,1,2,0:T(8,128)(2,1)S(1)}, bf16[1,26,1,256]{3,1,2,0:T(8,128)(2,1)S(1)}, u32[]{:S(2)}, u32[]{:S(2)}) collective-permute-start(bf16[1,26,1,256]{3,1,2,0:T(8,128)(2,1)S(1)} %get-tuple-element.114), channel_id=1, source_target_pairs={{4,0},{8,4},{12,8},{5,1},{9,5},{13,9},{6,2},{10,6},{14,10},{7,3},{... | collective-permute-start | bytes 39944 | tf_op jit(solution)/shard_map/while/body/eval_jaxpr/ppermute | solution.py:27
  72.8 6.5 %collective-permute-start = (bf16[1,1,24,256]{3,1,2,0:T(2,128)(2,1)S(1)}, bf16[1,1,24,256]{3,1,2,0:T(2,128)(2,1)S(1)}, u32[]{:S(2)}, u32[]{:S(2)}) collective-permute-start(bf16[1,1,24,256]{3,1,2,0:T(2,128)(2,1)S(1)} %get-tuple-element.112), channel_id=1, source_target_pairs={{1,0},{2,1},{3,2},{5,4},{6,5},{7,6},{9,8},{10,9},{11,10},{13,12},{... | collective-permute-start | bytes 36872 | tf_op jit(solution)/shard_map/while/body/eval_jaxpr/ppermute | solution.py:24
  80.2 6.6 %collective-permute-start.2 = (bf16[1,26,1,256]{3,1,2,0:T(8,128)(2,1)S(1)}, bf16[1,26,1,256]{3,1,2,0:T(8,128)(2,1)S(1)}, u32[]{:S(2)}, u32[]{:S(2)}) collective-permute-start(bf16[1,26,1,256]{3,1,2,0:T(8,128)(2,1)S(1)} %get-tuple-element.114), channel_id=1, source_target_pairs={{4,0},{8,4},{12,8},{5,1},{9,5},{13,9},{6,2},{10,6},{14,10},{7,3},{... | collective-permute-start | bytes 39944 | tf_op jit(solution)/shard_map/while/body/eval_jaxpr/ppermute | solution.py:27
  97.1 6.5 %collective-permute-start = (bf16[1,1,24,256]{3,1,2,0:T(2,128)(2,1)S(1)}, bf16[1,1,24,256]{3,1,2,0:T(2,128)(2,1)S(1)}, u32[]{:S(2)}, u32[]{:S(2)}) collective-permute-start(bf16[1,1,24,256]{3,1,2,0:T(2,128)(2,1)S(1)} %get-tuple-element.112), channel_id=1, source_target_pairs={{1,0},{2,1},{3,2},{5,4},{6,5},{7,6},{9,8},{10,9},{11,10},{13,12},{... | collective-permute-start | bytes 36872 | tf_op jit(solution)/shard_map/while/body/eval_jaxpr/ppermute | solution.py:24
  104.4 6.6 %collective-permute-start.2 = (bf16[1,26,1,256]{3,1,2,0:T(8,128)(2,1)S(1)}, bf16[1,26,1,256]{3,1,2,0:T(8,128)(2,1)S(1)}, u32[]{:S(2)}, u32[]{:S(2)}) collective-permute-start(bf16[1,26,1,256]{3,1,2,0:T(8,128)(2,1)S(1)} %get-tuple-element.114), channel_id=1, source_target_pairs={{4,0},{8,4},{12,8},{5,1},{9,5},{13,9},{6,2},{10,6},{14,10},{7,3},{... | collective-permute-start | bytes 39944 | tf_op jit(solution)/shard_map/while/body/eval_jaxpr/ppermute | solution.py:27
  121.3 6.5 %collective-permute-start = (bf16[1,1,24,256]{3,1,2,0:T(2,128)(2,1)S(1)}, bf16[1,1,24,256]{3,1,2,0:T(2,128)(2,1)S(1)}, u32[]{:S(2)}, u32[]{:S(2)}) collective-permute-start(bf16[1,1,24,256]{3,1,2,0:T(2,128)(2,1)S(1)} %get-tuple-element.112), channel_id=1, source_target_pairs={{1,0},{2,1},{3,2},{5,4},{6,5},{7,6},{9,8},{10,9},{11,10},{13,12},{... | collective-permute-start | bytes 36872 | tf_op jit(solution)/shard_map/while/body/eval_jaxpr/ppermute | solution.py:24
  122.6 6.1 %collective-permute-start.1 = (bf16[1,1,24,256]{3,1,2,0:T(2,128)(2,1)S(1)}, bf16[1,1,24,256]{3,1,2,0:T(2,128)(2,1)S(1)}, u32[]{:S(2)}, u32[]{:S(2)}) collective-permute-start(bf16[1,1,24,256]{3,1,2,0:T(2,128)(2,1)S(1)} %get-tuple-element.113), channel_id=1, source_target_pairs={{0,1},{1,2},{2,3},{4,5},{5,6},{6,7},{8,9},{9,10},{10,11},{12,13},{... | collective-permute-start | bytes 36872 | tf_op jit(solution)/shard_map/while/body/eval_jaxpr/ppermute | solution.py:23
  128.7 6.6 %collective-permute-start.2 = (bf16[1,26,1,256]{3,1,2,0:T(8,128)(2,1)S(1)}, bf16[1,26,1,256]{3,1,2,0:T(8,128)(2,1)S(1)}, u32[]{:S(2)}, u32[]{:S(2)}) collective-permute-start(bf16[1,26,1,256]{3,1,2,0:T(8,128)(2,1)S(1)} %get-tuple-element.114), channel_id=1, source_target_pairs={{4,0},{8,4},{12,8},{5,1},{9,5},{13,9},{6,2},{10,6},{14,10},{7,3},{... | collective-permute-start | bytes 39944 | tf_op jit(solution)/shard_map/while/body/eval_jaxpr/ppermute | solution.py:27
  145.6 6.5 %collective-permute-start = (bf16[1,1,24,256]{3,1,2,0:T(2,128)(2,1)S(1)}, bf16[1,1,24,256]{3,1,2,0:T(2,128)(2,1)S(1)}, u32[]{:S(2)}, u32[]{:S(2)}) collective-permute-start(bf16[1,1,24,256]{3,1,2,0:T(2,128)(2,1)S(1)} %get-tuple-element.112), channel_id=1, source_target_pairs={{1,0},{2,1},{3,2},{5,4},{6,5},{7,6},{9,8},{10,9},{11,10},{13,12},{... | collective-permute-start | bytes 36872 | tf_op jit(solution)/shard_map/while/body/eval_jaxpr/ppermute | solution.py:24
  146.9 6.1 %collective-permute-start.1 = (bf16[1,1,24,256]{3,1,2,0:T(2,128)(2,1)S(1)}, bf16[1,1,24,256]{3,1,2,0:T(2,128)(2,1)S(1)}, u32[]{:S(2)}, u32[]{:S(2)}) collective-permute-start(bf16[1,1,24,256]{3,1,2,0:T(2,128)(2,1)S(1)} %get-tuple-element.113), channel_id=1, source_target_pairs={{0,1},{1,2},{2,3},{4,5},{5,6},{6,7},{8,9},{9,10},{10,11},{12,13},{... | collective-permute-start | bytes 36872 | tf_op jit(solution)/shard_map/while/body/eval_jaxpr/ppermute | solution.py:23
  153.0 6.6 %collective-permute-start.2 = (bf16[1,26,1,256]{3,1,2,0:T(8,128)(2,1)S(1)}, bf16[1,26,1,256]{3,1,2,0:T(8,128)(2,1)S(1)}, u32[]{:S(2)}, u32[]{:S(2)}) collective-permute-start(bf16[1,26,1,256]{3,1,2,0:T(8,128)(2,1)S(1)} %get-tuple-element.114), channel_id=1, source_target_pairs={{4,0},{8,4},{12,8},{5,1},{9,5},{13,9},{6,2},{10,6},{14,10},{7,3},{... | collective-permute-start | bytes 39944 | tf_op jit(solution)/shard_map/while/body/eval_jaxpr/ppermute | solution.py:27
  169.8 6.5 %collective-permute-start = (bf16[1,1,24,256]{3,1,2,0:T(2,128)(2,1)S(1)}, bf16[1,1,24,256]{3,1,2,0:T(2,128)(2,1)S(1)}, u32[]{:S(2)}, u32[]{:S(2)}) collective-permute-start(bf16[1,1,24,256]{3,1,2,0:T(2,128)(2,1)S(1)} %get-tuple-element.112), channel_id=1, source_target_pairs={{1,0},{2,1},{3,2},{5,4},{6,5},{7,6},{9,8},{10,9},{11,10},{13,12},{... | collective-permute-start | bytes 36872 | tf_op jit(solution)/shard_map/while/body/eval_jaxpr/ppermute | solution.py:24
  171.1 6.1 %collective-permute-start.1 = (bf16[1,1,24,256]{3,1,2,0:T(2,128)(2,1)S(1)}, bf16[1,1,24,256]{3,1,2,0:T(2,128)(2,1)S(1)}, u32[]{:S(2)}, u32[]{:S(2)}) collective-permute-start(bf16[1,1,24,256]{3,1,2,0:T(2,128)(2,1)S(1)} %get-tuple-element.113), channel_id=1, source_target_pairs={{0,1},{1,2},{2,3},{4,5},{5,6},{6,7},{8,9},{9,10},{10,11},{12,13},{... | collective-permute-start | bytes 36872 | tf_op jit(solution)/shard_map/while/body/eval_jaxpr/ppermute | solution.py:23
  177.2 6.6 %collective-permute-start.2 = (bf16[1,26,1,256]{3,1,2,0:T(8,128)(2,1)S(1)}, bf16[1,26,1,256]{3,1,2,0:T(8,128)(2,1)S(1)}, u32[]{:S(2)}, u32[]{:S(2)}) collective-permute-start(bf16[1,26,1,256]{3,1,2,0:T(8,128)(2,1)S(1)} %get-tuple-element.114), channel_id=1, source_target_pairs={{4,0},{8,4},{12,8},{5,1},{9,5},{13,9},{6,2},{10,6},{14,10},{7,3},{... | collective-permute-start | bytes 39944 | tf_op jit(solution)/shard_map/while/body/eval_jaxpr/ppermute | solution.py:27
  194.1 6.5 %collective-permute-start = (bf16[1,1,24,256]{3,1,2,0:T(2,128)(2,1)S(1)}, bf16[1,1,24,256]{3,1,2,0:T(2,128)(2,1)S(1)}, u32[]{:S(2)}, u32[]{:S(2)}) collective-permute-start(bf16[1,1,24,256]{3,1,2,0:T(2,128)(2,1)S(1)} %get-tuple-element.112), channel_id=1, source_target_pairs={{1,0},{2,1},{3,2},{5,4},{6,5},{7,6},{9,8},{10,9},{11,10},{13,12},{... | collective-permute-start | bytes 36872 | tf_op jit(solution)/shard_map/while/body/eval_jaxpr/ppermute | solution.py:24
  195.4 6.1 %collective-permute-start.1 = (bf16[1,1,24,256]{3,1,2,0:T(2,128)(2,1)S(1)}, bf16[1,1,24,256]{3,1,2,0:T(2,128)(2,1)S(1)}, u32[]{:S(2)}, u32[]{:S(2)}) collective-permute-start(bf16[1,1,24,256]{3,1,2,0:T(2,128)(2,1)S(1)} %get-tuple-element.113), channel_id=1, source_target_pairs={{0,1},{1,2},{2,3},{4,5},{5,6},{6,7},{8,9},{9,10},{10,11},{12,13},{... | collective-permute-start | bytes 36872 | tf_op jit(solution)/shard_map/while/body/eval_jaxpr/ppermute | solution.py:23
  201.5 6.6 %collective-permute-start.2 = (bf16[1,26,1,256]{3,1,2,0:T(8,128)(2,1)S(1)}, bf16[1,26,1,256]{3,1,2,0:T(8,128)(2,1)S(1)}, u32[]{:S(2)}, u32[]{:S(2)}) collective-permute-start(bf16[1,26,1,256]{3,1,2,0:T(8,128)(2,1)S(1)} %get-tuple-element.114), channel_id=1, source_target_pairs={{4,0},{8,4},{12,8},{5,1},{9,5},{13,9},{6,2},{10,6},{14,10},{7,3},{... | collective-permute-start | bytes 39944 | tf_op jit(solution)/shard_map/while/body/eval_jaxpr/ppermute | solution.py:27
  218.4 6.5 %collective-permute-start = (bf16[1,1,24,256]{3,1,2,0:T(2,128)(2,1)S(1)}, bf16[1,1,24,256]{3,1,2,0:T(2,128)(2,1)S(1)}, u32[]{:S(2)}, u32[]{:S(2)}) collective-permute-start(bf16[1,1,24,256]{3,1,2,0:T(2,128)(2,1)S(1)} %get-tuple-element.112), channel_id=1, source_target_pairs={{1,0},{2,1},{3,2},{5,4},{6,5},{7,6},{9,8},{10,9},{11,10},{13,12},{... | collective-permute-start | bytes 36872 | tf_op jit(solution)/shard_map/while/body/eval_jaxpr/ppermute | solution.py:24
  219.7 6.1 %collective-permute-start.1 = (bf16[1,1,24,256]{3,1,2,0:T(2,128)(2,1)S(1)}, bf16[1,1,24,256]{3,1,2,0:T(2,128)(2,1)S(1)}, u32[]{:S(2)}, u32[]{:S(2)}) collective-permute-start(bf16[1,1,24,256]{3,1,2,0:T(2,128)(2,1)S(1)} %get-tuple-element.113), channel_id=1, source_target_pairs={{0,1},{1,2},{2,3},{4,5},{5,6},{6,7},{8,9},{9,10},{10,11},{12,13},{... | collective-permute-start | bytes 36872 | tf_op jit(solution)/shard_map/while/body/eval_jaxpr/ppermute | solution.py:23
  225.7 6.6 %collective-permute-start.2 = (bf16[1,26,1,256]{3,1,2,0:T(8,128)(2,1)S(1)}, bf16[1,26,1,256]{3,1,2,0:T(8,128)(2,1)S(1)}, u32[]{:S(2)}, u32[]{:S(2)}) collective-permute-start(bf16[1,26,1,256]{3,1,2,0:T(8,128)(2,1)S(1)} %get-tuple-element.114), channel_id=1, source_target_pairs={{4,0},{8,4},{12,8},{5,1},{9,5},{13,9},{6,2},{10,6},{14,10},{7,3},{... | collective-permute-start | bytes 39944 | tf_op jit(solution)/shard_map/while/body/eval_jaxpr/ppermute | solution.py:27
  242.6 6.5 %collective-permute-start = (bf16[1,1,24,256]{3,1,2,0:T(2,128)(2,1)S(1)}, bf16[1,1,24,256]{3,1,2,0:T(2,128)(2,1)S(1)}, u32[]{:S(2)}, u32[]{:S(2)}) collective-permute-start(bf16[1,1,24,256]{3,1,2,0:T(2,128)(2,1)S(1)} %get-tuple-element.112), channel_id=1, source_target_pairs={{1,0},{2,1},{3,2},{5,4},{6,5},{7,6},{9,8},{10,9},{11,10},{13,12},{... | collective-permute-start | bytes 36872 | tf_op jit(solution)/shard_map/while/body/eval_jaxpr/ppermute | solution.py:24
  243.9 6.1 %collective-permute-start.1 = (bf16[1,1,24,256]{3,1,2,0:T(2,128)(2,1)S(1)}, bf16[1,1,24,256]{3,1,2,0:T(2,128)(2,1)S(1)}, u32[]{:S(2)}, u32[]{:S(2)}) collective-permute-start(bf16[1,1,24,256]{3,1,2,0:T(2,128)(2,1)S(1)} %get-tuple-element.113), channel_id=1, source_target_pairs={{0,1},{1,2},{2,3},{4,5},{5,6},{6,7},{8,9},{9,10},{10,11},{12,13},{... | collective-permute-start | bytes 36872 | tf_op jit(solution)/shard_map/while/body/eval_jaxpr/ppermute | solution.py:23
  250.0 6.6 %collective-permute-start.2 = (bf16[1,26,1,256]{3,1,2,0:T(8,128)(2,1)S(1)}, bf16[1,26,1,256]{3,1,2,0:T(8,128)(2,1)S(1)}, u32[]{:S(2)}, u32[]{:S(2)}) collective-permute-start(bf16[1,26,1,256]{3,1,2,0:T(8,128)(2,1)S(1)} %get-tuple-element.114), channel_id=1, source_target_pairs={{4,0},{8,4},{12,8},{5,1},{9,5},{13,9},{6,2},{10,6},{14,10},{7,3},{... | collective-permute-start | bytes 39944 | tf_op jit(solution)/shard_map/while/body/eval_jaxpr/ppermute | solution.py:27
  266.9 6.5 %collective-permute-start = (bf16[1,1,24,256]{3,1,2,0:T(2,128)(2,1)S(1)}, bf16[1,1,24,256]{3,1,2,0:T(2,128)(2,1)S(1)}, u32[]{:S(2)}, u32[]{:S(2)}) collective-permute-start(bf16[1,1,24,256]{3,1,2,0:T(2,128)(2,1)S(1)} %get-tuple-element.112), channel_id=1, source_target_pairs={{1,0},{2,1},{3,2},{5,4},{6,5},{7,6},{9,8},{10,9},{11,10},{13,12},{... | collective-permute-start | bytes 36872 | tf_op jit(solution)/shard_map/while/body/eval_jaxpr/ppermute | solution.py:24
  268.2 6.1 %collective-permute-start.1 = (bf16[1,1,24,256]{3,1,2,0:T(2,128)(2,1)S(1)}, bf16[1,1,24,256]{3,1,2,0:T(2,128)(2,1)S(1)}, u32[]{:S(2)}, u32[]{:S(2)}) collective-permute-start(bf16[1,1,24,256]{3,1,2,0:T(2,128)(2,1)S(1)} %get-tuple-element.113), channel_id=1, source_target_pairs={{0,1},{1,2},{2,3},{4,5},{5,6},{6,7},{8,9},{9,10},{10,11},{12,13},{... | collective-permute-start | bytes 36872 | tf_op jit(solution)/shard_map/while/body/eval_jaxpr/ppermute | solution.py:23
  274.3 6.6 %collective-permute-start.2 = (bf16[1,26,1,256]{3,1,2,0:T(8,128)(2,1)S(1)}, bf16[1,26,1,256]{3,1,2,0:T(8,128)(2,1)S(1)}, u32[]{:S(2)}, u32[]{:S(2)}) collective-permute-start(bf16[1,26,1,256]{3,1,2,0:T(8,128)(2,1)S(1)} %get-tuple-element.114), channel_id=1, source_target_pairs={{4,0},{8,4},{12,8},{5,1},{9,5},{13,9},{6,2},{10,6},{14,10},{7,3},{... | collective-permute-start | bytes 39944 | tf_op jit(solution)/shard_map/while/body/eval_jaxpr/ppermute | solution.py:27
  291.1 6.5 %collective-permute-start = (bf16[1,1,24,256]{3,1,2,0:T(2,128)(2,1)S(1)}, bf16[1,1,24,256]{3,1,2,0:T(2,128)(2,1)S(1)}, u32[]{:S(2)}, u32[]{:S(2)}) collective-permute-start(bf16[1,1,24,256]{3,1,2,0:T(2,128)(2,1)S(1)} %get-tuple-element.112), channel_id=1, source_target_pairs={{1,0},{2,1},{3,2},{5,4},{6,5},{7,6},{9,8},{10,9},{11,10},{13,12},{... | collective-permute-start | bytes 36872 | tf_op jit(solution)/shard_map/while/body/eval_jaxpr/ppermute | solution.py:24
  292.4 6.1 %collective-permute-start.1 = (bf16[1,1,24,256]{3,1,2,0:T(2,128)(2,1)S(1)}, bf16[1,1,24,256]{3,1,2,0:T(2,128)(2,1)S(1)}, u32[]{:S(2)}, u32[]{:S(2)}) collective-permute-start(bf16[1,1,24,256]{3,1,2,0:T(2,128)(2,1)S(1)} %get-tuple-element.113), channel_id=1, source_target_pairs={{0,1},{1,2},{2,3},{4,5},{5,6},{6,7},{8,9},{9,10},{10,11},{12,13},{... | collective-permute-start | bytes 36872 | tf_op jit(solution)/shard_map/while/body/eval_jaxpr/ppermute | solution.py:23
  298.5 6.6 %collective-permute-start.2 = (bf16[1,26,1,256]{3,1,2,0:T(8,128)(2,1)S(1)}, bf16[1,26,1,256]{3,1,2,0:T(8,128)(2,1)S(1)}, u32[]{:S(2)}, u32[]{:S(2)}) collective-permute-start(bf16[1,26,1,256]{3,1,2,0:T(8,128)(2,1)S(1)} %get-tuple-element.114), channel_id=1, source_target_pairs={{4,0},{8,4},{12,8},{5,1},{9,5},{13,9},{6,2},{10,6},{14,10},{7,3},{... | collective-permute-start | bytes 39944 | tf_op jit(solution)/shard_map/while/body/eval_jaxpr/ppermute | solution.py:27
  315.4 6.5 %collective-permute-start = (bf16[1,1,24,256]{3,1,2,0:T(2,128)(2,1)S(1)}, bf16[1,1,24,256]{3,1,2,0:T(2,128)(2,1)S(1)}, u32[]{:S(2)}, u32[]{:S(2)}) collective-permute-start(bf16[1,1,24,256]{3,1,2,0:T(2,128)(2,1)S(1)} %get-tuple-element.112), channel_id=1, source_target_pairs={{1,0},{2,1},{3,2},{5,4},{6,5},{7,6},{9,8},{10,9},{11,10},{13,12},{... | collective-permute-start | bytes 36872 | tf_op jit(solution)/shard_map/while/body/eval_jaxpr/ppermute | solution.py:24
  316.7 6.1 %collective-permute-start.1 = (bf16[1,1,24,256]{3,1,2,0:T(2,128)(2,1)S(1)}, bf16[1,1,24,256]{3,1,2,0:T(2,128)(2,1)S(1)}, u32[]{:S(2)}, u32[]{:S(2)}) collective-permute-start(bf16[1,1,24,256]{3,1,2,0:T(2,128)(2,1)S(1)} %get-tuple-element.113), channel_id=1, source_target_pairs={{0,1},{1,2},{2,3},{4,5},{5,6},{6,7},{8,9},{9,10},{10,11},{12,13},{... | collective-permute-start | bytes 36872 | tf_op jit(solution)/shard_map/while/body/eval_jaxpr/ppermute | solution.py:23
  322.8 6.6 %collective-permute-start.2 = (bf16[1,26,1,256]{3,1,2,0:T(8,128)(2,1)S(1)}, bf16[1,26,1,256]{3,1,2,0:T(8,128)(2,1)S(1)}, u32[]{:S(2)}, u32[]{:S(2)}) collective-permute-start(bf16[1,26,1,256]{3,1,2,0:T(8,128)(2,1)S(1)} %get-tuple-element.114), channel_id=1, source_target_pairs={{4,0},{8,4},{12,8},{5,1},{9,5},{13,9},{6,2},{10,6},{14,10},{7,3},{... | collective-permute-start | bytes 39944 | tf_op jit(solution)/shard_map/while/body/eval_jaxpr/ppermute | solution.py:27
  339.7 6.5 %collective-permute-start = (bf16[1,1,24,256]{3,1,2,0:T(2,128)(2,1)S(1)}, bf16[1,1,24,256]{3,1,2,0:T(2,128)(2,1)S(1)}, u32[]{:S(2)}, u32[]{:S(2)}) collective-permute-start(bf16[1,1,24,256]{3,1,2,0:T(2,128)(2,1)S(1)} %get-tuple-element.112), channel_id=1, source_target_pairs={{1,0},{2,1},{3,2},{5,4},{6,5},{7,6},{9,8},{10,9},{11,10},{13,12},{... | collective-permute-start | bytes 36872 | tf_op jit(solution)/shard_map/while/body/eval_jaxpr/ppermute | solution.py:24
  341.0 6.1 %collective-permute-start.1 = (bf16[1,1,24,256]{3,1,2,0:T(2,128)(2,1)S(1)}, bf16[1,1,24,256]{3,1,2,0:T(2,128)(2,1)S(1)}, u32[]{:S(2)}, u32[]{:S(2)}) collective-permute-start(bf16[1,1,24,256]{3,1,2,0:T(2,128)(2,1)S(1)} %get-tuple-element.113), channel_id=1, source_target_pairs={{0,1},{1,2},{2,3},{4,5},{5,6},{6,7},{8,9},{9,10},{10,11},{12,13},{... | collective-permute-start | bytes 36872 | tf_op jit(solution)/shard_map/while/body/eval_jaxpr/ppermute | solution.py:23
  347.0 6.6 %collective-permute-start.2 = (bf16[1,26,1,256]{3,1,2,0:T(8,128)(2,1)S(1)}, bf16[1,26,1,256]{3,1,2,0:T(8,128)(2,1)S(1)}, u32[]{:S(2)}, u32[]{:S(2)}) collective-permute-start(bf16[1,26,1,256]{3,1,2,0:T(8,128)(2,1)S(1)} %get-tuple-element.114), channel_id=1, source_target_pairs={{4,0},{8,4},{12,8},{5,1},{9,5},{13,9},{6,2},{10,6},{14,10},{7,3},{... | collective-permute-start | bytes 39944 | tf_op jit(solution)/shard_map/while/body/eval_jaxpr/ppermute | solution.py:27
  363.9 6.5 %collective-permute-start = (bf16[1,1,24,256]{3,1,2,0:T(2,128)(2,1)S(1)}, bf16[1,1,24,256]{3,1,2,0:T(2,128)(2,1)S(1)}, u32[]{:S(2)}, u32[]{:S(2)}) collective-permute-start(bf16[1,1,24,256]{3,1,2,0:T(2,128)(2,1)S(1)} %get-tuple-element.112), channel_id=1, source_target_pairs={{1,0},{2,1},{3,2},{5,4},{6,5},{7,6},{9,8},{10,9},{11,10},{13,12},{... | collective-permute-start | bytes 36872 | tf_op jit(solution)/shard_map/while/body/eval_jaxpr/ppermute | solution.py:24
  365.2 6.1 %collective-permute-start.1 = (bf16[1,1,24,256]{3,1,2,0:T(2,128)(2,1)S(1)}, bf16[1,1,24,256]{3,1,2,0:T(2,128)(2,1)S(1)}, u32[]{:S(2)}, u32[]{:S(2)}) collective-permute-start(bf16[1,1,24,256]{3,1,2,0:T(2,128)(2,1)S(1)} %get-tuple-element.113), channel_id=1, source_target_pairs={{0,1},{1,2},{2,3},{4,5},{5,6},{6,7},{8,9},{9,10},{10,11},{12,13},{... | collective-permute-start | bytes 36872 | tf_op jit(solution)/shard_map/while/body/eval_jaxpr/ppermute | solution.py:23
  371.3 6.6 %collective-permute-start.2 = (bf16[1,26,1,256]{3,1,2,0:T(8,128)(2,1)S(1)}, bf16[1,26,1,256]{3,1,2,0:T(8,128)(2,1)S(1)}, u32[]{:S(2)}, u32[]{:S(2)}) collective-permute-start(bf16[1,26,1,256]{3,1,2,0:T(8,128)(2,1)S(1)} %get-tuple-element.114), channel_id=1, source_target_pairs={{4,0},{8,4},{12,8},{5,1},{9,5},{13,9},{6,2},{10,6},{14,10},{7,3},{... | collective-permute-start | bytes 39944 | tf_op jit(solution)/shard_map/while/body/eval_jaxpr/ppermute | solution.py:27
  388.2 6.5 %collective-permute-start = (bf16[1,1,24,256]{3,1,2,0:T(2,128)(2,1)S(1)}, bf16[1,1,24,256]{3,1,2,0:T(2,128)(2,1)S(1)}, u32[]{:S(2)}, u32[]{:S(2)}) collective-permute-start(bf16[1,1,24,256]{3,1,2,0:T(2,128)(2,1)S(1)} %get-tuple-element.112), channel_id=1, source_target_pairs={{1,0},{2,1},{3,2},{5,4},{6,5},{7,6},{9,8},{10,9},{11,10},{13,12},{... | collective-permute-start | bytes 36872 | tf_op jit(solution)/shard_map/while/body/eval_jaxpr/ppermute | solution.py:24
  389.5 6.1 %collective-permute-start.1 = (bf16[1,1,24,256]{3,1,2,0:T(2,128)(2,1)S(1)}, bf16[1,1,24,256]{3,1,2,0:T(2,128)(2,1)S(1)}, u32[]{:S(2)}, u32[]{:S(2)}) collective-permute-start(bf16[1,1,24,256]{3,1,2,0:T(2,128)(2,1)S(1)} %get-tuple-element.113), channel_id=1, source_target_pairs={{0,1},{1,2},{2,3},{4,5},{5,6},{6,7},{8,9},{9,10},{10,11},{12,13},{... | collective-permute-start | bytes 36872 | tf_op jit(solution)/shard_map/while/body/eval_jaxpr/ppermute | solution.py:23
  395.6 6.6 %collective-permute-start.2 = (bf16[1,26,1,256]{3,1,2,0:T(8,128)(2,1)S(1)}, bf16[1,26,1,256]{3,1,2,0:T(8,128)(2,1)S(1)}, u32[]{:S(2)}, u32[]{:S(2)}) collective-permute-start(bf16[1,26,1,256]{3,1,2,0:T(8,128)(2,1)S(1)} %get-tuple-element.114), channel_id=1, source_target_pairs={{4,0},{8,4},{12,8},{5,1},{9,5},{13,9},{6,2},{10,6},{14,10},{7,3},{... | collective-permute-start | bytes 39944 | tf_op jit(solution)/shard_map/while/body/eval_jaxpr/ppermute | solution.py:27
  412.5 6.5 %collective-permute-start = (bf16[1,1,24,256]{3,1,2,0:T(2,128)(2,1)S(1)}, bf16[1,1,24,256]{3,1,2,0:T(2,128)(2,1)S(1)}, u32[]{:S(2)}, u32[]{:S(2)}) collective-permute-start(bf16[1,1,24,256]{3,1,2,0:T(2,128)(2,1)S(1)} %get-tuple-element.112), channel_id=1, source_target_pairs={{1,0},{2,1},{3,2},{5,4},{6,5},{7,6},{9,8},{10,9},{11,10},{13,12},{... | collective-permute-start | bytes 36872 | tf_op jit(solution)/shard_map/while/body/eval_jaxpr/ppermute | solution.py:24
  413.8 6.1 %collective-permute-start.1 = (bf16[1,1,24,256]{3,1,2,0:T(2,128)(2,1)S(1)}, bf16[1,1,24,256]{3,1,2,0:T(2,128)(2,1)S(1)}, u32[]{:S(2)}, u32[]{:S(2)}) collective-permute-start(bf16[1,1,24,256]{3,1,2,0:T(2,128)(2,1)S(1)} %get-tuple-element.113), channel_id=1, source_target_pairs={{0,1},{1,2},{2,3},{4,5},{5,6},{6,7},{8,9},{9,10},{10,11},{12,13},{... | collective-permute-start | bytes 36872 | tf_op jit(solution)/shard_map/while/body/eval_jaxpr/ppermute | solution.py:23
  419.8 6.6 %collective-permute-start.2 = (bf16[1,26,1,256]{3,1,2,0:T(8,128)(2,1)S(1)}, bf16[1,26,1,256]{3,1,2,0:T(8,128)(2,1)S(1)}, u32[]{:S(2)}, u32[]{:S(2)}) collective-permute-start(bf16[1,26,1,256]{3,1,2,0:T(8,128)(2,1)S(1)} %get-tuple-element.114), channel_id=1, source_target_pairs={{4,0},{8,4},{12,8},{5,1},{9,5},{13,9},{6,2},{10,6},{14,10},{7,3},{... | collective-permute-start | bytes 39944 | tf_op jit(solution)/shard_map/while/body/eval_jaxpr/ppermute | solution.py:27
  436.7 6.5 %collective-permute-start = (bf16[1,1,24,256]{3,1,2,0:T(2,128)(2,1)S(1)}, bf16[1,1,24,256]{3,1,2,0:T(2,128)(2,1)S(1)}, u32[]{:S(2)}, u32[]{:S(2)}) collective-permute-start(bf16[1,1,24,256]{3,1,2,0:T(2,128)(2,1)S(1)} %get-tuple-element.112), channel_id=1, source_target_pairs={{1,0},{2,1},{3,2},{5,4},{6,5},{7,6},{9,8},{10,9},{11,10},{13,12},{... | collective-permute-start | bytes 36872 | tf_op jit(solution)/shard_map/while/body/eval_jaxpr/ppermute | solution.py:24
  438.0 6.1 %collective-permute-start.1 = (bf16[1,1,24,256]{3,1,2,0:T(2,128)(2,1)S(1)}, bf16[1,1,24,256]{3,1,2,0:T(2,128)(2,1)S(1)}, u32[]{:S(2)}, u32[]{:S(2)}) collective-permute-start(bf16[1,1,24,256]{3,1,2,0:T(2,128)(2,1)S(1)} %get-tuple-element.113), channel_id=1, source_target_pairs={{0,1},{1,2},{2,3},{4,5},{5,6},{6,7},{8,9},{9,10},{10,11},{12,13},{... | collective-permute-start | bytes 36872 | tf_op jit(solution)/shard_map/while/body/eval_jaxpr/ppermute | solution.py:23
  444.1 6.6 %collective-permute-start.2 = (bf16[1,26,1,256]{3,1,2,0:T(8,128)(2,1)S(1)}, bf16[1,26,1,256]{3,1,2,0:T(8,128)(2,1)S(1)}, u32[]{:S(2)}, u32[]{:S(2)}) collective-permute-start(bf16[1,26,1,256]{3,1,2,0:T(8,128)(2,1)S(1)} %get-tuple-element.114), channel_id=1, source_target_pairs={{4,0},{8,4},{12,8},{5,1},{9,5},{13,9},{6,2},{10,6},{14,10},{7,3},{... | collective-permute-start | bytes 39944 | tf_op jit(solution)/shard_map/while/body/eval_jaxpr/ppermute | solution.py:27
  461.0 6.5 %collective-permute-start = (bf16[1,1,24,256]{3,1,2,0:T(2,128)(2,1)S(1)}, bf16[1,1,24,256]{3,1,2,0:T(2,128)(2,1)S(1)}, u32[]{:S(2)}, u32[]{:S(2)}) collective-permute-start(bf16[1,1,24,256]{3,1,2,0:T(2,128)(2,1)S(1)} %get-tuple-element.112), channel_id=1, source_target_pairs={{1,0},{2,1},{3,2},{5,4},{6,5},{7,6},{9,8},{10,9},{11,10},{13,12},{... | collective-permute-start | bytes 36872 | tf_op jit(solution)/shard_map/while/body/eval_jaxpr/ppermute | solution.py:24
  468.3 6.6 %collective-permute-start.2 = (bf16[1,26,1,256]{3,1,2,0:T(8,128)(2,1)S(1)}, bf16[1,26,1,256]{3,1,2,0:T(8,128)(2,1)S(1)}, u32[]{:S(2)}, u32[]{:S(2)}) collective-permute-start(bf16[1,26,1,256]{3,1,2,0:T(8,128)(2,1)S(1)} %get-tuple-element.114), channel_id=1, source_target_pairs={{4,0},{8,4},{12,8},{5,1},{9,5},{13,9},{6,2},{10,6},{14,10},{7,3},{... | collective-permute-start | bytes 39944 | tf_op jit(solution)/shard_map/while/body/eval_jaxpr/ppermute | solution.py:27
  485.2 6.5 %collective-permute-start = (bf16[1,1,24,256]{3,1,2,0:T(2,128)(2,1)S(1)}, bf16[1,1,24,256]{3,1,2,0:T(2,128)(2,1)S(1)}, u32[]{:S(2)}, u32[]{:S(2)}) collective-permute-start(bf16[1,1,24,256]{3,1,2,0:T(2,128)(2,1)S(1)} %get-tuple-element.112), channel_id=1, source_target_pairs={{1,0},{2,1},{3,2},{5,4},{6,5},{7,6},{9,8},{10,9},{11,10},{13,12},{... | collective-permute-start | bytes 36872 | tf_op jit(solution)/shard_map/while/body/eval_jaxpr/ppermute | solution.py:24
  492.6 6.6 %collective-permute-start.2 = (bf16[1,26,1,256]{3,1,2,0:T(8,128)(2,1)S(1)}, bf16[1,26,1,256]{3,1,2,0:T(8,128)(2,1)S(1)}, u32[]{:S(2)}, u32[]{:S(2)}) collective-permute-start(bf16[1,26,1,256]{3,1,2,0:T(8,128)(2,1)S(1)} %get-tuple-element.114), channel_id=1, source_target_pairs={{4,0},{8,4},{12,8},{5,1},{9,5},{13,9},{6,2},{10,6},{14,10},{7,3},{... | collective-permute-start | bytes 39944 | tf_op jit(solution)/shard_map/while/body/eval_jaxpr/ppermute | solution.py:27
  509.5 6.5 %collective-permute-start = (bf16[1,1,24,256]{3,1,2,0:T(2,128)(2,1)S(1)}, bf16[1,1,24,256]{3,1,2,0:T(2,128)(2,1)S(1)}, u32[]{:S(2)}, u32[]{:S(2)}) collective-permute-start(bf16[1,1,24,256]{3,1,2,0:T(2,128)(2,1)S(1)} %get-tuple-element.112), channel_id=1, source_target_pairs={{1,0},{2,1},{3,2},{5,4},{6,5},{7,6},{9,8},{10,9},{11,10},{13,12},{... | collective-permute-start | bytes 36872 | tf_op jit(solution)/shard_map/while/body/eval_jaxpr/ppermute | solution.py:24
  510.8 6.1 %collective-permute-start.1 = (bf16[1,1,24,256]{3,1,2,0:T(2,128)(2,1)S(1)}, bf16[1,1,24,256]{3,1,2,0:T(2,128)(2,1)S(1)}, u32[]{:S(2)}, u32[]{:S(2)}) collective-permute-start(bf16[1,1,24,256]{3,1,2,0:T(2,128)(2,1)S(1)} %get-tuple-element.113), channel_id=1, source_target_pairs={{0,1},{1,2},{2,3},{4,5},{5,6},{6,7},{8,9},{9,10},{10,11},{12,13},{... | collective-permute-start | bytes 36872 | tf_op jit(solution)/shard_map/while/body/eval_jaxpr/ppermute | solution.py:23
  516.9 6.6 %collective-permute-start.2 = (bf16[1,26,1,256]{3,1,2,0:T(8,128)(2,1)S(1)}, bf16[1,26,1,256]{3,1,2,0:T(8,128)(2,1)S(1)}, u32[]{:S(2)}, u32[]{:S(2)}) collective-permute-start(bf16[1,26,1,256]{3,1,2,0:T(8,128)(2,1)S(1)} %get-tuple-element.114), channel_id=1, source_target_pairs={{4,0},{8,4},{12,8},{5,1},{9,5},{13,9},{6,2},{10,6},{14,10},{7,3},{... | collective-permute-start | bytes 39944 | tf_op jit(solution)/shard_map/while/body/eval_jaxpr/ppermute | solution.py:27
  533.8 6.5 %collective-permute-start = (bf16[1,1,24,256]{3,1,2,0:T(2,128)(2,1)S(1)}, bf16[1,1,24,256]{3,1,2,0:T(2,128)(2,1)S(1)}, u32[]{:S(2)}, u32[]{:S(2)}) collective-permute-start(bf16[1,1,24,256]{3,1,2,0:T(2,128)(2,1)S(1)} %get-tuple-element.112), channel_id=1, source_target_pairs={{1,0},{2,1},{3,2},{5,4},{6,5},{7,6},{9,8},{10,9},{11,10},{13,12},{... | collective-permute-start | bytes 36872 | tf_op jit(solution)/shard_map/while/body/eval_jaxpr/ppermute | solution.py:24
  541.1 6.6 %collective-permute-start.2 = (bf16[1,26,1,256]{3,1,2,0:T(8,128)(2,1)S(1)}, bf16[1,26,1,256]{3,1,2,0:T(8,128)(2,1)S(1)}, u32[]{:S(2)}, u32[]{:S(2)}) collective-permute-start(bf16[1,26,1,256]{3,1,2,0:T(8,128)(2,1)S(1)} %get-tuple-element.114), channel_id=1, source_target_pairs={{4,0},{8,4},{12,8},{5,1},{9,5},{13,9},{6,2},{10,6},{14,10},{7,3},{... | collective-permute-start | bytes 39944 | tf_op jit(solution)/shard_map/while/body/eval_jaxpr/ppermute | solution.py:27
  558.0 6.5 %collective-permute-start = (bf16[1,1,24,256]{3,1,2,0:T(2,128)(2,1)S(1)}, bf16[1,1,24,256]{3,1,2,0:T(2,128)(2,1)S(1)}, u32[]{:S(2)}, u32[]{:S(2)}) collective-permute-start(bf16[1,1,24,256]{3,1,2,0:T(2,128)(2,1)S(1)} %get-tuple-element.112), channel_id=1, source_target_pairs={{1,0},{2,1},{3,2},{5,4},{6,5},{7,6},{9,8},{10,9},{11,10},{13,12},{... | collective-permute-start | bytes 36872 | tf_op jit(solution)/shard_map/while/body/eval_jaxpr/ppermute | solution.py:24
  565.4 6.6 %collective-permute-start.2 = (bf16[1,26,1,256]{3,1,2,0:T(8,128)(2,1)S(1)}, bf16[1,26,1,256]{3,1,2,0:T(8,128)(2,1)S(1)}, u32[]{:S(2)}, u32[]{:S(2)}) collective-permute-start(bf16[1,26,1,256]{3,1,2,0:T(8,128)(2,1)S(1)} %get-tuple-element.114), channel_id=1, source_target_pairs={{4,0},{8,4},{12,8},{5,1},{9,5},{13,9},{6,2},{10,6},{14,10},{7,3},{... | collective-permute-start | bytes 39944 | tf_op jit(solution)/shard_map/while/body/eval_jaxpr/ppermute | solution.py:27
  (56 other events, 549.3 us)
where the time goes:
time: 592 us; the launch traced here: 583 us
  starting transfers between devices  293 us (49%)
  matrix products  136 us (23%)
  local copies, waits for them, and re-layouts  83 us (14%)
  waiting for transfers between devices  35.4 us (6%)
  other arithmetic  31.5 us (5%)
    conv_general_dilated x24, matrix products, one_step(): lax.conv_general_dilated(padded, w_rec, (1, 1), 'VALID', dimension_number...  136 us
    ppermute x24, starting transfers between devices, with_halo(): from_above = lax.ppermute(tile[:, -1:], 'rows', rows_down)  121 us
    ppermute x24, starting transfers between devices, with_halo(): from_left = lax.ppermute(tall_tile[:, :, -1:], 'cols', cols_right)  110 us
    ppermute x24, starting transfers between devices, with_halo(): from_below = lax.ppermute(tile[:, :1], 'rows', rows_up)  31 us
    ppermute x24, starting transfers between devices, with_halo(): from_right = lax.ppermute(tall_tile[:, :, :1], 'cols', cols_left)  31 us
    div x48, local copies, waits for them, and re-layouts, lstm_update(): jax.nn.sigmoid(forget_gate) * c_prev  22.1 us
    ppermute x24, waiting for transfers between devices, with_halo(): from_above = lax.ppermute(tile[:, -1:], 'rows', rows_down)  19.7 us
    dynamic_update_slice x24, local copies, waits for them, and re-layouts, device_fn(): final_state, h_seq = lax.scan(one_step, (h_init, c_init), gate_bias)  18.6 us
  transfers between devices with their start and end apart: 96, of which 48 were waited for; matrix products, arithmetic and copies ran while one was open for 3% of the time, Pallas kernels for 0%

commit v1 on v0

v1 whole, which is shorter than its diff:
```python
import functools

import jax
import jax.numpy as jnp
from jax import lax
from jax.experimental import pallas as pl
from jax.experimental.pallas import tpu as pltpu
from jax.sharding import PartitionSpec as P

T = 24
CH = 256
PITCH = 29
ROWS = 34
MESH = pl.DeviceIdType.MESH
DIRS = ((-1, 0), (0, -1), (-1, -1), (-1, 1), (1, -1), (1, 1), (0, 1), (1, 0))


def addr(h, w):
    return 2 * ((h + 2) * PITCH + (w + 2))


def cells(piece, dh=0, dw=0):
    kind, h, w, n = piece
    stride = 2 if kind == "H" else 2 * PITCH
    return pl.ds(addr(h + dh, w + dw), 8 * n, stride=stride)


IN1 = [("V", 1, w, 2) for w in range(1, 23)] + [p for h in range(17, 23) for p in (("H", h, 1, 2), ("H", h, 15, 1))]
RIM1 = [("V", 1, w, 3) for w in (-1, 0, 23, 24)]
RIM1 += [p for h in (-1, 0) for p in (("H", h, -1, 3), ("H", h, 17, 1))]
RIM1 += [p for h in (23, 24) for p in (("H", h, 1, 2), ("H", h, 15, 1))]
RIM2 = [("H", h, 0, 3) for h in (0, 1, 18, 19, 20, 21, 22, 23)] + [("V", 2, w, 2) for w in (0, 1, 22, 23)]
IN2 = [("V", 2, w, 2) for w in range(2, 22)]

TAPS = [(dh, dw) for dh in (-1, 0, 1) for dw in (-1, 0, 1)]
KTILES = [((2 * k, 0), (2 * k + 1, 0)) for k in range(4)] + [((8, 0), (8, 1))]
KTILES += [((2 * k, 1), (2 * k + 1, 1)) for k in range(4)]


def split8(block):
    out = []
    for kind, h, w, n in block:
        for g in range(n):
            out.append((kind, h + 8 * g, w, 1) if kind == "V" else (kind, h, w + 8 * g, 1))
    return out


def kernel(steps, row_count, col_count, h_in, c_in, w_in, bias, h_out, c_out, *scratch):
    (he, ho, ce, co, mask, wts, pack, c_stage, col_send, cor_send, crow_send, ccor_send,
     hline, hcor, cline, ccor, load_sem, out_sem, send_sem, recv_sem) = scratch
    dp = lax.axis_index("dp")
    col = lax.axis_index("cols")
    row = lax.axis_index("rows")

    def has(k):
        dr, dc = DIRS[k]
        ok = jnp.int32(1)
        if dr:
            ok = ok * jnp.where((row > 0) if dr < 0 else (row < row_count - 1), 1, 0)
        if dc:
            ok = ok * jnp.where((col > 0) if dc < 0 else (col < col_count - 1), 1, 0)
        return ok

    present = [has(k) for k in range(8)]

    def target(k):
        dr, dc = DIRS[k]
        ok = present[k]
        return (jnp.where(ok == 1, dp, 1 - dp), col + ok * dc, row + ok * dr), jnp.where(ok == 1, 7 - k, k)

    loads = []
    for p in range(2):
        for gate in range(4):
            loads.append(pltpu.make_async_copy(
                w_in.at[:, :, pl.ds(gate * CH + p * 128, 128)],
                wts.at[p, :, :, pl.ds(gate * 128, 128)], load_sem.at[2 + p * 4 + gate]))
    h_load = pltpu.make_async_copy(h_in, pack.at[1], load_sem.at[0])
    c_load = pltpu.make_async_copy(c_in, c_stage, load_sem.at[1])
    h_load.start()
    c_load.start()
    for ld in loads:
        ld.start()

    barrier = pltpu.get_barrier_semaphore()
    for k in range(8):
        dev, _ = target(k)
        pl.semaphore_signal(barrier, inc=1, device_id=dev, device_id_type=MESH)

    hmin, hmax = -present[0], T - 1 + present[7]
    wmin, wmax = -present[1], T - 1 + present[6]
    for piece in split8(RIM1):
        kind, h, w, _ = piece
        line = lax.broadcasted_iota(jnp.int32, (8, 128), 0)
        hh = line + h if kind == "V" else jnp.full((8, 128), h, jnp.int32)
        ww = line + w if kind == "H" else jnp.full((8, 128), w, jnp.int32)
        inside = (hh >= hmin) & (hh <= hmax) & (ww >= wmin) & (ww <= wmax)
        mask[cells(piece), :] = jnp.where(inside, 1.0, 0.0)

    h_load.wait()
    for h in range(0, T, 2):
        val = pack[1, pl.ds(h * T, 2 * T), :].astype(jnp.float32)
        for s in range(2):
            for p in range(2):
                he[p][cells(("H", h + s, 0, 3)), :] = val[s * T:(s + 1) * T, p * 128:(p + 1) * 128]
    c_load.wait()
    for h in range(T):
        for p in range(2):
            ce[p][cells(("H", h, 0, 3)), :] = c_stage[pl.ds(h * T, T), pl.ds(p * 128, 128)]

    def both(bufs, piece):
        return jnp.concatenate([bufs[0][cells(piece), :], bufs[1][cells(piece), :]], axis=1)

    def pack_rows(bufs, slot, h):
        val = jnp.concatenate([both(bufs, ("H", h, 0, 3)), both(bufs, ("H", h + 1, 0, 3))], axis=0)
        pack[slot, pl.ds(h * T, 2 * T), :] = val.astype(jnp.bfloat16)

    def pack_sends():
        for j, w in enumerate((0, 22)):
            val = jnp.concatenate([both(he, ("V", 0, w, 3)), both(he, ("V", 0, w + 1, 3))], axis=0)
            col_send[j] = val.astype(jnp.bfloat16)
        for j, (h, w) in enumerate(((0, 0), (0, 22), (22, 0), (22, 22))):
            val = jnp.concatenate([both(he, ("V", h, w, 1)), both(he, ("V", h, w + 1, 1))], axis=0)
            cor_send[j] = val.astype(jnp.bfloat16)
        for j, piece in enumerate((("H", 0, 0, 3), ("V", 0, 0, 3), ("V", 0, 23, 3), ("H", 23, 0, 3))):
            crow_send[j] = both(ce, piece)
        for j, (h, w) in enumerate(((0, 0), (0, 23), (23, 0), (23, 23))):
            ccor_send[j] = both(ce, ("V", h, w, 1))

    def copy(k, n, slot, dev, there):
        dr, dc = DIRS[k]
        if dr and dc:
            j = (0 if dr < 0 else 2) + (0 if dc < 0 else 1)
            pairs = ((cor_send.at[j], hcor.at[slot, there]), (ccor_send.at[j], ccor.at[slot, there]))
        else:
            j = {0: 0, 1: 1, 6: 2, 7: 3}[k]
            if dr:
                src = pack.at[1, pl.ds(0 if dr < 0 else (T - 2) * T, 2 * T)]
            else:
                src = col_send.at[0 if dc < 0 else 1]
            pairs = ((src, hline.at[slot, there]), (crow_send.at[j], cline.at[slot, there]))
        return pltpu.make_async_remote_copy(
            src_ref=pairs[n][0], dst_ref=pairs[n][1], send_sem=send_sem.at[k, n],
            recv_sem=recv_sem.at[slot, there, n], device_id=dev, device_id_type=MESH)

    ORDER = (2, 3, 4, 5, 1, 6, 0, 7)

    def start_sends(slot):
        for n in range(2):
            for k in ORDER:
                dev, there = target(k)
                copy(k, n, slot, dev, there).start()

    def wait_sends(slot):
        for k in range(8):
            dev, there = target(k)
            for n in range(2):
                copy(k, n, slot, dev, there).wait_send()

    def wait_recvs(slot):
        for k in range(8):
            dev, _ = target(k)
            for n in range(2):
                copy(7 - k, n, slot, dev, k).wait_recv()

    def unpack(slot):
        for k in range(8):
            dr, dc = DIRS[k]
            ok = present[k] == 1
            if dr and dc:
                val = jnp.where(ok, hcor[slot, k].astype(jnp.float32), 0.0)
                h, w = (-2 if dr < 0 else T), (-2 if dc < 0 else T)
                for s in range(2):
                    for p in range(2):
                        he[p][pl.ds(addr(h, w + s), 2, stride=2 * PITCH), :] = val[8 * s:8 * s + 2, p * 128:(p + 1) * 128]
                cval = ccor[slot, k]
                h, w = (-1 if dr < 0 else T), (-1 if dc < 0 else T)
                for p in range(2):
                    ce[p][pl.ds(addr(h, w), 1), :] = cval[0:1, p * 128:(p + 1) * 128]
            else:
                val = jnp.where(ok, hline[slot, k].astype(jnp.float32), 0.0)
                cval = cline[slot, k]
                for s in range(2):
                    piece = ("H", (-2 if dr < 0 else T) + s, 0, 3) if dr else ("V", 0, (-2 if dc < 0 else T) + s, 3)
                    for p in range(2):
                        he[p][cells(piece), :] = val[s * T:(s + 1) * T, p * 128:(p + 1) * 128]
                piece = ("H", -1 if dr < 0 else T, 0, 3) if dr else ("V", 0, -1 if dc < 0 else T, 3)
                for p in range(2):
                    ce[p][cells(piece), :] = cval[:, p * 128:(p + 1) * 128]

    pack_sends()
    pl.semaphore_wait(barrier, 8)
    start_sends(0)
    for ld in loads:
        ld.wait()

    def rhs(p, k):
        parts = [wts[p, tap, pl.ds(half * 128, 128), :] for tap, half in KTILES[k]]
        return jnp.concatenate(parts, axis=0)

    def lhs_of(bufs, block, k):
        parts = []
        for tap, half in KTILES[k]:
            dh, dw = TAPS[tap]
            parts.append(jnp.concatenate([bufs[half][cells(piece, dh, dw), :] for piece in block], axis=0))
        return jnp.concatenate(parts, axis=1).astype(jnp.bfloat16)

    def epilogue(i, p, pair, gates, c_src, c_dst, h_dst, step_bias, masked):
        b_i, b_f, b_o, b_g = (step_bias[gate * 2 + p] for gate in range(4))
        for s, piece in enumerate(pair):
            v = gates[16 * i + 8 * s:16 * i + 8 * s + 8]
            in_gate = 0.5 * jnp.tanh(0.5 * (v[:, :128] + b_i)) + 0.5
            forget = 0.5 * jnp.tanh(0.5 * (v[:, 128:256] + b_f)) + 0.5
            out_gate = 0.5 * jnp.tanh(0.5 * (v[:, 256:384] + b_o)) + 0.5
            cand = jnp.tanh(v[:, 384:] + b_g)
            c_new = forget * c_src[p][cells(piece), :] + in_gate * cand
            c_dst[p][cells(piece), :] = c_new
            h_new = (out_gate * jnp.tanh(c_new)).astype(jnp.bfloat16).astype(jnp.float32)
            if masked:
                h_new = h_new * mask[cells(piece), :]
            h_dst[p][cells(piece), :] = h_new

    def pair_steps(n, _):
        slot = lax.rem(n, 2)
        biases = []
        for s in range(2):
            line = bias[pl.ds(2 * n + s, 1), :]
            biases.append([jnp.broadcast_to(line[:, j * 128:(j + 1) * 128], (8, 128)) for j in range(8)])
        first = (he, ho, ce, co, biases[0])
        second = (ho, he, co, ce, biases[1])
        plan = [(IN1, first, False), (RIM1, first, True), (RIM2, second, False), (IN2, second, False)]
        stages = [(b, p) for b in range(4) for p in range(2)]
        odd_out = pltpu.make_async_copy(pack.at[0], h_out.at[2 * n], out_sem.at[0])
        even_out = pltpu.make_async_copy(pack.at[1], h_out.at[2 * n + 1], out_sem.at[1])
        todo = []
        for idx, (b, p) in enumerate(stages):
            block, (src, h_dst, c_src, c_dst, step_bias), masked = plan[b]
            groups = split8(block)
            if (b, p) == (1, 0):
                wait_recvs(slot)
                unpack(slot)
            if (b, p) == (2, 1):
                @pl.when(n > 0)
                def _():
                    odd_out.wait()
            per_tile = -(-len(todo) // 4)
            gates = None
            for k in range(9):
                part = jnp.dot(lhs_of(src, block, k), rhs(p, k), preferred_element_type=jnp.float32)
                gates = part if gates is None else gates + part
                for unit in todo[:per_tile]:
                    unit()
                todo = todo[per_tile:]
                if (b, p) == (2, 1) and k >= 3:
                    for h in range(4 * (k - 3), min(4 * (k - 3) + 4, T), 2):
                        pack_rows(ho, 0, h)
                if (b, p) == (3, 0) and k == 4:
                    odd_out.start()
                    @pl.when(n > 0)
                    def _():
                        even_out.wait()
                    wait_sends(slot)
                    pack_rows(he, 1, 0)
                    pack_rows(he, 1, T - 2)
                    pack_sends()
                    start_sends(1 - slot)
            todo = [functools.partial(epilogue, i, p, groups[2 * i:2 * i + 2], gates, c_src, c_dst, h_dst, step_bias, masked)
                    for i in range(len(groups) // 2)]
        for unit in todo:
            unit()
        for h in range(2, T - 2, 2):
            pack_rows(he, 1, h)
        even_out.start()
        return 0

    lax.fori_loop(0, steps // 2, pair_steps, 0)

    for h in range(T):
        c_stage[pl.ds(h * T, T), :] = both(ce, ("H", h, 0, 3))
    c_save = pltpu.make_async_copy(c_stage, c_out, load_sem.at[1])
    c_save.start()
    last = steps // 2
    wait_recvs(last % 2)
    wait_sends(last % 2)
    for s in range(2):
        pltpu.make_async_copy(pack.at[s], h_out.at[steps - 2 + s], out_sem.at[s]).wait()
    c_save.wait()


def solution(mesh):
    row_count = mesh.shape["rows"]
    col_count = mesh.shape["cols"]
    assert mesh.shape["dp"] == 2

    def device_fn(h_init, c_init, w_rec, gate_bias):
        steps = gate_bias.shape[0]
        assert h_init.shape == (1, T, T, CH) and steps % 2 == 0
        cell_rows = 2 * ROWS * PITCH
        f32, bf16 = jnp.float32, jnp.bfloat16
        plane = [pltpu.VMEM((cell_rows, 128), f32)] * 2
        hbm = pl.BlockSpec(memory_space=pl.ANY)
        scratch = [
            plane, plane, plane, plane,
            pltpu.VMEM((cell_rows, 128), f32),
            pltpu.VMEM((2, 9, 256, 512), bf16),
            pltpu.VMEM((2, T * T, CH), bf16),
            pltpu.VMEM((T * T, CH), f32),
            pltpu.VMEM((2, 2 * T, CH), bf16),
            pltpu.VMEM((4, 16, CH), bf16),
            pltpu.VMEM((4, T, CH), f32),
            pltpu.VMEM((4, 8, CH), f32),
            pltpu.VMEM((2, 8, 2 * T, CH), bf16),
            pltpu.VMEM((2, 8, 16, CH), bf16),
            pltpu.VMEM((2, 8, T, CH), f32),
            pltpu.VMEM((2, 8, 8, CH), f32),
            pltpu.SemaphoreType.DMA((10,)),
            pltpu.SemaphoreType.DMA((2,)),
            pltpu.SemaphoreType.DMA((8, 2)),
            pltpu.SemaphoreType.DMA((2, 8, 2)),
        ]
        flat, shapes = [], []
        for s in scratch:
            shapes.append(len(s) if isinstance(s, list) else 0)
            flat += s if isinstance(s, list) else [s]

        def body(*refs):
            args, rest = refs[:6], list(refs[6:])
            grouped = []
            for count in shapes:
                if count:
                    grouped.append([rest.pop(0) for _ in range(count)])
                else:
                    grouped.append(rest.pop(0))
            kernel(steps, row_count, col_count, *args, *grouped)

        h_seq, c_last = pl.pallas_call(
            body,
            out_shape=(jax.ShapeDtypeStruct((steps, T * T, CH), bf16), jax.ShapeDtypeStruct((T * T, CH), f32)),
            in_specs=[hbm, hbm, hbm, pl.BlockSpec(memory_space=pltpu.VMEM)],
            out_specs=(hbm, hbm),
            scratch_shapes=flat,
            compiler_params=pltpu.CompilerParams(collective_id=0, has_side_effects=True, vmem_limit_bytes=48 * 1024 * 1024),
            name="conv_lstm",
        )(h_init.reshape(T * T, CH), c_init.reshape(T * T, CH), w_rec.reshape(9, CH, 4 * CH), gate_bias)
        return h_seq.reshape(steps, 1, T, T, CH), c_last.reshape(1, T, T, CH)

    state_spec = P("dp", "rows", "cols", None)
    return jax.shard_map(device_fn, mesh=mesh, in_specs=(state_spec, state_spec, P(), P()), out_specs=(P(None, "dp", "rows", "cols", None), state_spec), check_vma=False)
```

time: 592 us -> 110 us (0.19); the launches traced: 583 us -> 109 us
  starting transfers between devices: 293 us -> 0 us
  matrix products: 136 us -> 0 us
  Pallas kernels: 0 us -> 98.4 us
  local copies, waits for them, and re-layouts: 83 us -> 10.4 us
  waiting for transfers between devices: 35.4 us -> 0 us
  other arithmetic: 31.5 us -> 0 us
    ppermute x96 -> x0, starting transfers between devices: 293 us -> none  [the longest x24 121 us: with_halo(): from_above = lax.ppermute(tile[:, -1:], 'rows', rows_down)]
    conv_general_dilated x24 -> x0, matrix products: 136 us -> none  [one_step(): lax.conv_general_dilated(padded, w_rec, (1, 1), 'VALID', dimension_number...]
    pallas_call x0 -> x1, Pallas kernels: none -> 98.4 us  [device_fn(): pl.pallas_call(body, out_shape=(jax.ShapeDtypeStruct((steps, T * T, CH),...]
    ppermute x96 -> x0, waiting for transfers between devices: 35.4 us -> none  [the longest x24 19.7 us: with_halo(): from_above = lax.ppermute(tile[:, -1:], 'rows', rows_down)]
    div x48 -> x0, local copies, waits for them, and re-layouts: 22.1 us -> none  [lstm_update(): jax.nn.sigmoid(forget_gate) * c_prev]
    dynamic_update_slice x24 -> x0, local copies, waits for them, and re-layouts: 18.6 us -> none  [device_fn(): final_state, h_seq = lax.scan(one_step, (h_init, c_init), gate_bias)]
    dynamic_slice x24 -> x0, local copies, waits for them, and re-layouts: 18.5 us -> none  [device_fn(): final_state, h_seq = lax.scan(one_step, (h_init, c_init), gate_bias)]
    div x24 -> x0, other arithmetic: 17.3 us -> none  [lstm_update(): jax.nn.sigmoid(forget_gate) * c_prev]
  transfers between devices with their start and end apart: 96 -> 0, of which waited for: 48 -> 0; matrix products, arithmetic and copies ran while one was open for 3% -> 0% of each run, Pallas kernels for 0% -> 0%
where the time goes in v1:
time: 110 us; the launch traced here: 109 us
  Pallas kernels  98.4 us (89%)
  local copies, waits for them, and re-layouts  10.4 us (9%)
    pallas_call x1, Pallas kernels, device_fn(): pl.pallas_call(body, out_shape=(jax.ShapeDtypeStruct((steps, T * T, CH),...  98.4 us
    unnamed x8, local copies, waits for them, and re-layouts  10.4 us

profile of v1, /device:TPU:0, one launch (start us, length us, event | category | flops | bytes accessed | tf_op | source)
XLA Modules:
  0.0 109.4 jit_solution(2491714269598886062)
XLA Ops:
  0.6 0.0 copy-start
  0.6 1.1 copy-done
  1.7 0.0 copy-start.1
  1.7 1.0 copy-done.1
  2.7 0.0 copy-start.2
  2.7 0.9 copy-done.2
  3.6 98.4 %conv_lstm.1 = (bf16[24,576,256]{2,1,0:T(8,128)(2,1)}, f32[576,256]{1,0:T(8,128)S(1)}) custom-call(bf16[576,256]{1,0:T(8,128)(2,1)S(1)} %bitcast.9, f32[576,256]{1,0:T(8,128)S(1)} %bitcast.8, bf16[9,256,1024]{2,1,0:T(8,128)(2,1)} %bitcast.11, f32[24,1024]{1,0:T(8,128)S(1)} %copy-done.2), custom_call_target="tpu_custom_call" | custom-call | tf_op jit(solution)/shard_map/conv_lstm/pallas_call | solution.py:335
  102.0 6.7 %copy.9 = bf16[24,1,24,24,256]{4,3,2,1,0:T(8,128)(2,1)} copy(bf16[24,1,24,24,256]{4,3,2,1,0:T(8,128)(2,1)} %bitcast.10) | data formatting | bytes 14155776
  108.6 0.8 copy.10
Async XLA Ops:
  0.6 1.1 copy-start
  1.7 1.0 copy-start.1
  2.7 0.9 copy-start.2

commit v2 on v1

v2 whole, which is shorter than its diff:
```python
import functools

import jax
import jax.numpy as jnp
from jax import lax
from jax.experimental import pallas as pl
from jax.experimental.pallas import tpu as pltpu
from jax.sharding import PartitionSpec as P

T = 24
CH = 256
PITCH = 29
ROWS = 34
MESH = pl.DeviceIdType.MESH
DIRS = ((-1, 0), (0, -1), (-1, -1), (-1, 1), (1, -1), (1, 1), (0, 1), (1, 0))


def addr(h, w):
    return 2 * ((h + 2) * PITCH + (w + 2))


def cells(piece, dh=0, dw=0):
    kind, h, w, n = piece
    stride = 2 if kind == "H" else 2 * PITCH
    return pl.ds(addr(h + dh, w + dw), 8 * n, stride=stride)


IN1 = [("V", 1, w, 2) for w in range(1, 23)] + [p for h in range(17, 23) for p in (("H", h, 1, 2), ("H", h, 15, 1))]
RIM1 = [("V", 1, w, 3) for w in (-1, 0, 23, 24)]
RIM1 += [p for h in (-1, 0) for p in (("H", h, -1, 3), ("H", h, 17, 1))]
RIM1 += [p for h in (23, 24) for p in (("H", h, 1, 2), ("H", h, 15, 1))]
RIM2 = [("H", h, 0, 3) for h in (0, 1, 18, 19, 20, 21, 22, 23)] + [("V", 2, w, 2) for w in (0, 1, 22, 23)]
IN2 = [("V", 2, w, 2) for w in range(2, 22)]

TAPS = [(dh, dw) for dh in (-1, 0, 1) for dw in (-1, 0, 1)]
KTILES = [((2 * k, 0), (2 * k + 1, 0)) for k in range(4)] + [((8, 0), (8, 1))]
KTILES += [((2 * k, 1), (2 * k + 1, 1)) for k in range(4)]


def split8(block):
    out = []
    for kind, h, w, n in block:
        for g in range(n):
            out.append((kind, h + 8 * g, w, 1) if kind == "V" else (kind, h, w + 8 * g, 1))
    return out


def kernel(steps, row_count, col_count, h_in, c_in, w_in, bias_in, h_out, c_out, *scratch):
    (he, hr, ho, ce, co, mask, wts, bias, h_stage, c_stage, row_send, col_send, cline_send, cor_send,
     hline, cline, corner, load_sem, send_sem, recv_sem) = scratch
    dp = lax.axis_index("dp")
    col = lax.axis_index("cols")
    row = lax.axis_index("rows")

    def has(k):
        dr, dc = DIRS[k]
        ok = jnp.int32(1)
        if dr:
            ok = ok * jnp.where((row > 0) if dr < 0 else (row < row_count - 1), 1, 0)
        if dc:
            ok = ok * jnp.where((col > 0) if dc < 0 else (col < col_count - 1), 1, 0)
        return ok

    present = [has(k) for k in range(8)]

    def target(k):
        dr, dc = DIRS[k]
        ok = present[k]
        return (jnp.where(ok == 1, dp, 1 - dp), col + ok * dc, row + ok * dr), jnp.where(ok == 1, 7 - k, k)

    loads = []
    for p in range(2):
        for gate in range(4):
            loads.append(pltpu.make_async_copy(
                w_in.at[:, :, pl.ds(gate * CH + p * 128, 128)],
                wts.at[p, :, :, pl.ds(gate * 128, 128)], load_sem.at[2 + p * 4 + gate]))
    h_load = pltpu.make_async_copy(h_in, h_stage, load_sem.at[0])
    c_load = pltpu.make_async_copy(c_in, c_stage, load_sem.at[1])
    loads.append(pltpu.make_async_copy(bias_in, bias, load_sem.at[10]))
    h_load.start()
    c_load.start()
    for ld in loads:
        ld.start()

    barrier = pltpu.get_barrier_semaphore()
    for k in range(8):
        dev, _ = target(k)
        pl.semaphore_signal(barrier, inc=1, device_id=dev, device_id_type=MESH)

    hmin, hmax = -present[0], T - 1 + present[7]
    wmin, wmax = -present[1], T - 1 + present[6]
    for piece in split8(RIM1):
        kind, h, w, _ = piece
        line = lax.broadcasted_iota(jnp.int32, (8, 128), 0)
        hh = line + h if kind == "V" else jnp.full((8, 128), h, jnp.int32)
        ww = line + w if kind == "H" else jnp.full((8, 128), w, jnp.int32)
        inside = (hh >= hmin) & (hh <= hmax) & (ww >= wmin) & (ww <= wmax)
        mask[cells(piece), :] = jnp.where(inside, 1.0, 0.0)

    h_load.wait()
    for h in range(0, T, 2):
        val = h_stage[pl.ds(h * T, 2 * T), :].astype(jnp.float32)
        for s in range(2):
            for p in range(2):
                part = val[s * T:(s + 1) * T, p * 128:(p + 1) * 128]
                he[p][cells(("H", h + s, 0, 3)), :] = part
                hr[p][cells(("H", h + s, 0, 3)), :] = part
    c_load.wait()
    for h in range(T):
        for p in range(2):
            ce[p][cells(("H", h, 0, 3)), :] = c_stage[pl.ds(h * T, T), pl.ds(p * 128, 128)]

    def both(bufs, piece):
        return jnp.concatenate([bufs[0][cells(piece), :], bufs[1][cells(piece), :]], axis=1)

    def two_lines(bufs, first, second):
        return jnp.concatenate([both(bufs, first), both(bufs, second)], axis=0).astype(jnp.bfloat16)

    def pack_rows(bufs, t, h):
        h_out[t, pl.ds(h * T, 2 * T), :] = two_lines(bufs, ("H", h, 0, 3), ("H", h + 1, 0, 3))

    def pack_sends():
        for j, h in enumerate((0, 22)):
            row_send[j] = two_lines(hr, ("H", h, 0, 3), ("H", h + 1, 0, 3))
        for j, w in enumerate((0, 22)):
            col_send[j] = two_lines(hr, ("V", 0, w, 3), ("V", 0, w + 1, 3))
        for j, (h, w) in enumerate(((0, 0), (0, 22), (22, 0), (22, 22))):
            for p in range(2):
                lanes = pl.ds(p * 128, 128)
                for s in range(2):
                    cor_send[j, pl.ds(2 * s, 2), lanes] = hr[p][pl.ds(addr(h, w + s), 2, stride=2 * PITCH), :]
                cor_send[j, pl.ds(4, 1), lanes] = ce[p][pl.ds(addr(h and T - 1, w and T - 1), 1), :]
        for j, piece in enumerate((("H", 0, 0, 3), ("V", 0, 0, 3), ("V", 0, 23, 3), ("H", 23, 0, 3))):
            cline_send[j] = both(ce, piece)

    LINES = (1, 6, 0, 7)
    CORNERS = (2, 3, 4, 5)
    MESSAGES = [(k, 0) for k in CORNERS + LINES] + [(k, 1) for k in LINES]

    def copy(k, n, slot, dev, there):
        dr, dc = DIRS[k]
        if dr and dc:
            src, dst = cor_send.at[(0 if dr < 0 else 2) + (0 if dc < 0 else 1)], corner.at[slot, there]
        elif n:
            src, dst = cline_send.at[{0: 0, 1: 1, 6: 2, 7: 3}[k]], cline.at[slot, there]
        else:
            src, dst = (row_send.at[0 if dr < 0 else 1] if dr else col_send.at[0 if dc < 0 else 1]), hline.at[slot, there]
        return pltpu.make_async_remote_copy(
            src_ref=src, dst_ref=dst, send_sem=send_sem.at[k, n], recv_sem=recv_sem.at[slot, there, n],
            device_id=dev, device_id_type=MESH)

    def start_sends(slot):
        for k, n in MESSAGES:
            dev, there = target(k)
            copy(k, n, slot, dev, there).start()

    def wait_sends(slot):
        for k, n in MESSAGES:
            dev, there = target(k)
            copy(k, n, slot, dev, there).wait_send()

    def wait_recvs(slot, part):
        for k, n in MESSAGES:
            if n == part:
                dev, _ = target(k)
                copy(7 - k, n, slot, dev, k).wait_recv()

    def unpack_h(slot):
        for k in range(8):
            dr, dc = DIRS[k]
            ok = present[k] == 1
            if dr and dc:
                val = jnp.where(ok, corner[slot, k], 0.0)
                h, w = (-2 if dr < 0 else T), (-2 if dc < 0 else T)
                for s in range(2):
                    for p in range(2):
                        hr[p][pl.ds(addr(h, w + s), 2, stride=2 * PITCH), :] = val[2 * s:2 * s + 2, p * 128:(p + 1) * 128]
            else:
                val = jnp.where(ok, hline[slot, k].astype(jnp.float32), 0.0)
                for s in range(2):
                    piece = ("H", (-2 if dr < 0 else T) + s, 0, 3) if dr else ("V", 0, (-2 if dc < 0 else T) + s, 3)
                    for p in range(2):
                        hr[p][cells(piece), :] = val[s * T:(s + 1) * T, p * 128:(p + 1) * 128]

    def unpack_c(slot):
        for k in range(8):
            dr, dc = DIRS[k]
            h, w = (-1 if dr < 0 else T), (-1 if dc < 0 else T)
            for p in range(2):
                lanes = pl.ds(p * 128, 128)
                if dr and dc:
                    ce[p][pl.ds(addr(h, w), 1), :] = corner[slot, k, pl.ds(4, 1), lanes]
                else:
                    piece = ("H", h, 0, 3) if dr else ("V", 0, w, 3)
                    ce[p][cells(piece), :] = cline[slot, k, :, lanes]

    pack_sends()
    pl.semaphore_wait(barrier, 8)
    start_sends(0)
    for ld in loads:
        ld.wait()

    def rhs(p, k):
        parts = [wts[p, tap, pl.ds(half * 128, 128), :] for tap, half in KTILES[k]]
        return jnp.concatenate(parts, axis=0)

    def lhs_of(bufs, block, k):
        parts = []
        for tap, half in KTILES[k]:
            dh, dw = TAPS[tap]
            parts.append(jnp.concatenate([bufs[half][cells(piece, dh, dw), :] for piece in block], axis=0))
        return jnp.concatenate(parts, axis=1).astype(jnp.bfloat16)

    def epilogue(i, p, pair, gates, c_src, c_dst, h_dst, step_bias, rim):
        b_i, b_f, b_o, b_g = (step_bias[gate * 2 + p] for gate in range(4))
        for s, piece in enumerate(pair):
            v = gates[16 * i + 8 * s:16 * i + 8 * s + 8]
            in_gate = 0.5 * jnp.tanh(0.5 * (v[:, :128] + b_i)) + 0.5
            forget = 0.5 * jnp.tanh(0.5 * (v[:, 128:256] + b_f)) + 0.5
            out_gate = 0.5 * jnp.tanh(0.5 * (v[:, 256:384] + b_o)) + 0.5
            cand = jnp.tanh(v[:, 384:] + b_g)
            c_new = forget * c_src[p][cells(piece), :] + in_gate * cand
            c_dst[p][cells(piece), :] = c_new
            h_new = (out_gate * jnp.tanh(c_new)).astype(jnp.bfloat16).astype(jnp.float32)
            if rim == 1:
                h_new = h_new * mask[cells(piece), :]
            h_dst[p][cells(piece), :] = h_new
            if rim == 2 and (piece[0] == "V" or piece[1] in (0, 1, 22, 23) or piece[2] in (0, 16)):
                hr[p][cells(piece), :] = h_new

    def pair_steps(n, _):
        slot = lax.rem(n, 2)
        biases = []
        for s in range(2):
            line = bias[pl.ds(2 * n + s, 1), :]
            biases.append([jnp.broadcast_to(line[:, j * 128:(j + 1) * 128], (8, 128)) for j in range(8)])
        first = (ho, ce, co, biases[0])
        second = (he, co, ce, biases[1])
        plan = [(IN1, he, first, 0), (RIM1, hr, first, 1), (RIM2, ho, second, 2), (IN2, ho, second, 0)]
        todo = []
        for b, p in ((b, p) for b in range(4) for p in range(2)):
            block, src, (h_dst, c_src, c_dst, step_bias), rim = plan[b]
            groups = split8(block)
            per_tile = -(-len(todo) // 4)
            gates = None
            for k in range(9):
                part = jnp.dot(lhs_of(src, block, k), rhs(p, k), preferred_element_type=jnp.float32)
                gates = part if gates is None else gates + part
                for unit in todo[:per_tile]:
                    unit()
                todo = todo[per_tile:]
                if (b, p, k) == (0, 1, 7):
                    wait_recvs(slot, 0)
                    unpack_h(slot)
                if (b, p, k) == (1, 0, 5):
                    wait_recvs(slot, 1)
                    unpack_c(slot)
                if (b, p) == (2, 1) and k >= 3:
                    for h in range(4 * (k - 3), min(4 * (k - 3) + 4, T), 2):
                        pack_rows(ho, 2 * n, h)
                if (b, p, k) == (3, 0, 4):
                    wait_sends(slot)
                    pack_sends()

                    @pl.when(n < steps // 2 - 1)
                    def _():
                        start_sends(1 - slot)
            todo = [functools.partial(epilogue, i, p, groups[2 * i:2 * i + 2], gates, c_src, c_dst, h_dst, step_bias, rim)
                    for i in range(len(groups) // 2)]
        for unit in todo:
            unit()
        for h in range(0, T, 2):
            pack_rows(he, 2 * n + 1, h)
        return 0

    lax.fori_loop(0, steps // 2, pair_steps, 0)

    for h in range(T):
        c_stage[pl.ds(h * T, T), :] = both(ce, ("H", h, 0, 3))
    c_save = pltpu.make_async_copy(c_stage, c_out, load_sem.at[1])
    c_save.start()
    c_save.wait()


def solution(mesh):
    row_count = mesh.shape["rows"]
    col_count = mesh.shape["cols"]
    assert mesh.shape["dp"] == 2

    def device_fn(h_init, c_init, w_rec, gate_bias):
        steps = gate_bias.shape[0]
        assert h_init.shape == (1, T, T, CH) and steps % 2 == 0
        cell_rows = 2 * ROWS * PITCH
        f32, bf16 = jnp.float32, jnp.bfloat16
        plane = [pltpu.VMEM((cell_rows, 128), f32)] * 2
        hbm = pl.BlockSpec(memory_space=pltpu.HBM)
        vmem = pl.BlockSpec(memory_space=pltpu.VMEM)
        scratch = [
            plane, plane, plane, plane, plane,
            pltpu.VMEM((cell_rows, 128), f32),
            pltpu.VMEM((2, 9, 256, 512), bf16),
            pltpu.VMEM((steps, 4 * CH), f32),
            pltpu.VMEM((T * T, CH), bf16),
            pltpu.VMEM((T * T, CH), f32),
            pltpu.VMEM((2, 2 * T, CH), bf16),
            pltpu.VMEM((2, 2 * T, CH), bf16),
            pltpu.VMEM((4, T, CH), f32),
            pltpu.VMEM((4, 8, CH), f32),
            pltpu.VMEM((2, 8, 2 * T, CH), bf16),
            pltpu.VMEM((2, 8, T, CH), f32),
            pltpu.VMEM((2, 8, 8, CH), f32),
            pltpu.SemaphoreType.DMA((11,)),
            pltpu.SemaphoreType.DMA((8, 2)),
            pltpu.SemaphoreType.DMA((2, 8, 2)),
        ]
        flat, shapes = [], []
        for s in scratch:
            shapes.append(len(s) if isinstance(s, list) else 0)
            flat += s if isinstance(s, list) else [s]

        def body(*refs):
            args, rest = refs[:6], list(refs[6:])
            grouped = []
            for count in shapes:
                if count:
                    grouped.append([rest.pop(0) for _ in range(count)])
                else:
                    grouped.append(rest.pop(0))
            kernel(steps, row_count, col_count, *args, *grouped)

        h_seq, c_last = pl.pallas_call(
            body,
            out_shape=(jax.ShapeDtypeStruct((steps, T * T, CH), bf16), jax.ShapeDtypeStruct((T * T, CH), f32)),
            in_specs=[hbm] * 4,
            out_specs=(vmem, hbm),
            scratch_shapes=flat,
            compiler_params=pltpu.CompilerParams(collective_id=0, has_side_effects=True, vmem_limit_bytes=40 * 1024 * 1024),
            name="conv_lstm",
        )(*(pltpu.with_memory_space_constraint(x, pltpu.HBM) for x in (h_init.reshape(T * T, CH), c_init.reshape(T * T, CH), w_rec.reshape(9, CH, 4 * CH), gate_bias)))
        return h_seq.reshape(steps, 1, T, T, CH), c_last.reshape(1, T, T, CH)

    state_spec = P("dp", "rows", "cols", None)
    return jax.shard_map(device_fn, mesh=mesh, in_specs=(state_spec, state_spec, P(), P()), out_specs=(P(None, "dp", "rows", "cols", None), state_spec), check_vma=False)
```

time: 110 us -> 97 us (0.88)
  local copies, waits for them, and re-layouts: 10.4 us -> 3.78 us
  Pallas kernels: 98.4 us -> 92.4 us
    unnamed x8 -> x2, local copies, waits for them, and re-layouts: 10.4 us -> 3.78 us
    pallas_call x1, Pallas kernels: 98.4 us -> 92.4 us  [device_fn(): pl.pallas_call(body, out_shape=(jax.ShapeDtypeStruct((steps, T * T, CH),...]
where the time goes in v2:
time: 97 us; the launch traced here: 96.8 us
  Pallas kernels  92.4 us (95%)
  local copies, waits for them, and re-layouts  3.78 us (4%)
    pallas_call x1, Pallas kernels, device_fn(): pl.pallas_call(body, out_shape=(jax.ShapeDtypeStruct((steps, T * T, CH),...  92.4 us
    unnamed x2, local copies, waits for them, and re-layouts  3.78 us

profile of v2, /device:TPU:0, one launch (start us, length us, event | category | flops | bytes accessed | tf_op | source)
XLA Modules:
  0.0 96.8 jit_solution(6846304477181878500)
XLA Ops:
  0.6 92.4 %conv_lstm.1 = (bf16[24,576,256]{2,1,0:T(8,128)(2,1)S(1)}, f32[576,256]{1,0:T(8,128)S(1)}) custom-call(bf16[576,256]{1,0:T(8,128)(2,1)} %bitcast.11, f32[576,256]{1,0:T(8,128)} %bitcast.10, bf16[9,256,1024]{2,1,0:T(8,128)(2,1)} %bitcast.9, f32[24,1024]{1,0:T(8,128)} %refs_3_.1), custom_call_target="tpu_custom_call" | custom-call | tf_op jit(solution)/shard_map/conv_lstm/pallas_call | solution.py:331
  93.1 3.0 %copy.9 = bf16[24,1,24,24,256]{4,3,2,1,0:T(8,128)(2,1)} copy(bf16[24,1,24,24,256]{4,3,2,1,0:T(8,128)(2,1)S(1)} %bitcast.7) | data formatting | bytes 14155776
  96.0 0.8 copy.10
